TPU v7x, 256 devices: a whole 4x4x8 slice. The times are simulated.
256 devices in a mesh: dp: 4 (over y), expert: 32 (over x, z), etp: 2 (over core).
Axes of the slice: x: 4, y: 4, z: 8, core: 2. Of those that a mesh axis runs over, the one named last changes fastest.
Arguments:
- tokens: bfloat16 [8192, 4096], P(('dp', 'expert'), 'etp'), may hold values from -6 to 6
- expert_ids: int32 [8192, 8], P(('dp', 'expert')), may hold values from 0 to 63, all different within a row; in each aligned block of 64 rows (0 to 63, 64 to 127, ...) at most 12 rows name the same one
- combine: float32 [8192, 8], P(('dp', 'expert')), may hold values from 0.05 to 1
- gate_weight: bfloat16 [64, 4096, 1536], P('expert', 'dp', 'etp'), may hold values from -0.09375 to 0.09375
- up_weight: bfloat16 [64, 4096, 1536], P('expert', 'dp', 'etp'), may hold values from -0.09375 to 0.09375
- down_weight: bfloat16 [64, 1536, 4096], P('expert', 'etp', 'dp'), may hold values from -0.15625 to 0.15625
Outputs:
- mixed: bfloat16 [8192, 4096], P(('dp', 'expert'), 'etp')
Inputs may be any that keep to these rules, and one draw needn't show every extreme that they name: `expert_ids`: each row names 8 different experts. In the rows of one device (aligned blocks of 64 rows) no expert is named by more than 12 rows, a bound that some block reaches.
All inputs are finite; a program needn't handle non-finite values.
Results may differ from a plain program's by a relative error of at most 0.008.
Values may be sent and summed in bfloat16 or wider, within the bound.
No kernel may reach another device: no remote copies, remote signals or barrier semaphores. Data moves between devices by JAX's collectives and lax.ppermute only.
A program may use at most 192 MiB of HBM per device.

v0:
```python
import jax
import jax.numpy as jnp
from jax import lax
from jax.sharding import PartitionSpec as P


def sent_to_all(shard, axis):
    copies = jnp.broadcast_to(shard, (lax.axis_size(axis), *shard.shape))
    return lax.all_to_all(copies, axis, split_axis=0, concat_axis=0, tiled=True)


def laid_out(pieces, dim):
    pieces = jnp.moveaxis(pieces, 0, dim)
    dims = pieces.shape
    return pieces.reshape(*dims[:dim], dims[dim] * dims[dim + 1], *dims[dim + 2 :])


def gather_directly(shard, axis, dim):
    pieces = sent_to_all(shard, axis)
    return laid_out(pieces, dim)


def in_one_piece(arrays, axis, dim, along):
    widths = [a.shape[along] for a in arrays]
    both = jnp.concatenate(arrays, axis=along)
    filled = lax.all_gather(both, axis, axis=dim, tiled=True)
    return tuple(jnp.split(filled, [sum(widths[:k]) for k in range(1, len(widths))], axis=along))


def cut_along(shard, dim, count):
    before, after = (shard.shape[:dim], shard.shape[dim + 1 :])
    return jnp.moveaxis(shard.reshape(*before, count, -1, *after), dim, 0)


def sum_at_owner(shard, axis, dim):
    count = lax.axis_size(axis)
    pieces = lax.all_to_all(cut_along(shard, dim, count), axis, 0, 0, tiled=True)
    return jnp.sum(pieces.astype(jnp.float32), axis=0)


def shards(tokens, expert_ids, combine, gate_weight, up_weight, down_weight):
    tok_rows, top_count = expert_ids.shape
    held_count = gate_weight.shape[0]
    groups = lax.axis_size("expert")
    experts = held_count * groups
    capacity = min(tok_rows, 3 * tok_rows * top_count // (2 * experts))
    slots_all = experts * capacity
    onehot = (expert_ids[:, :, None] == jnp.arange(experts, dtype=jnp.int32)[None, None, :]).astype(
        jnp.int32
    )
    flattened = onehot.reshape(tok_rows * top_count, experts)
    before = jnp.cumsum(flattened, axis=0) - flattened
    slot_index = jnp.sum(before * flattened, axis=1).reshape(tok_rows, top_count)
    target = expert_ids * capacity + slot_index
    matches = target[:, :, None] == jnp.arange(slots_all, dtype=jnp.int32)[None, None, :]
    picker = jnp.any(matches, axis=1).astype(jnp.bfloat16)
    weights_map = jnp.sum(jnp.where(matches, combine[:, :, None], 0.0), axis=1)
    gathered = gather_directly(tokens, "etp", 1)
    packed = jnp.einsum("ts,td->sd", picker, gathered, preferred_element_type=jnp.float32).astype(
        jnp.bfloat16
    )
    arrived = lax.all_to_all(
        packed.reshape(groups, held_count, capacity, gathered.shape[1]),
        "expert",
        split_axis=0,
        concat_axis=2,
        tiled=True,
    )
    inputs = arrived[0]
    pieces = in_one_piece((gate_weight, up_weight), "dp", 1, 0)
    gate_part = jnp.einsum("erd,edf->erf", inputs, pieces[0], preferred_element_type=jnp.float32)
    up_part = jnp.einsum("erd,edf->erf", inputs, pieces[1], preferred_element_type=jnp.float32)
    hidden = (jax.nn.silu(gate_part) * up_part).astype(jnp.bfloat16)
    partial_value = jnp.einsum(
        "erf,efd->erd",
        hidden,
        lax.all_gather(down_weight, "dp", axis=2, tiled=True),
        preferred_element_type=jnp.float32,
    ).astype(jnp.bfloat16)
    partial_value = lax.optimization_barrier(partial_value)
    summed = sum_at_owner(partial_value.astype(jnp.float32).astype(jnp.bfloat16), "etp", 2)
    expert_out = summed.astype(jnp.bfloat16)
    returned_rows = lax.all_to_all(
        expert_out[None], "expert", split_axis=2, concat_axis=0, tiled=True
    )
    returned_rows = returned_rows.reshape(slots_all, returned_rows.shape[3])
    weight_high = weights_map.astype(jnp.bfloat16)
    weight_low = (weights_map - weight_high.astype(jnp.float32)).astype(jnp.bfloat16)
    result = jnp.dot(weight_high, returned_rows, preferred_element_type=jnp.float32)
    result = result + jnp.dot(weight_low, returned_rows, preferred_element_type=jnp.float32)
    return result.astype(jnp.bfloat16)


def solution(mesh):
    placed = (
        P(("dp", "expert"), "etp"),
        P(("dp", "expert"), None),
        P(("dp", "expert"), None),
        P("expert", "dp", "etp"),
        P("expert", "dp", "etp"),
        P("expert", "etp", "dp"),
    )
    return jax.shard_map(
        shards, mesh=mesh, in_specs=placed, out_specs=P(("dp", "expert"), "etp"), check_vma=False
    )
```

profile of v0, /device:TPU:8, one launch (start us, length us, event | category | flops | bytes accessed | tf_op | source)
XLA Modules:
  0.0 497.5 jit_solution(5117173287641867535)
XLA Ops:
  6.5 6.0 %pad_maximum_fusion = bf16[4,1024,768]{2,1,0:T(8,128)(2,1)} fusion(bf16[2,1024,768]{2,1,0:T(8,128)(2,1)} %param.10, bf16[2,1024,768]{2,1,0:T(8,128)(2,1)} %param.9), kind=kLoop, calls=%fused_computation.7 | loop fusion | flops 3145728 | bytes 12582912 | tf_op jit(solution)/shard_map/concatenate | solution.py:25
  12.6 0.7 all-gather.5.cloned.1.call-update
  13.5 0.9 broadcast_in_dim.25
  14.4 3.5 all-to-all-start
  18.2 1.2 reduce-window.6
  20.6 4.4 convolution_convert_fusion.1
  25.1 10.3 %reshape.40 = bf16[32,2,12,4096]{3,2,1,0:T(8,128)(2,1)} reshape(bf16[768,4096]{1,0:T(8,128)(2,1)} %convolution_convert_fusion.1) | data formatting | bytes 12582912 | tf_op jit(solution)/shard_map/reshape | solution.py:63
  35.3 9.9 %copy.54 = bf16[32,2,12,4096]{3,1,2,0:T(2,128)(2,1)S(1)} copy(bf16[32,2,12,4096]{3,2,1,0:T(8,128)(2,1)} %reshape.40) | data formatting | bytes 12582912 | tf_op jit(solution)/shard_map/reshape | solution.py:63
  45.2 153.1 %all_to_all.40 = bf16[32,2,12,4096]{3,1,2,0:T(2,128)(2,1)} all-to-all(bf16[32,2,12,4096]{3,1,2,0:T(2,128)(2,1)S(1)} %copy.54), channel_id=1, replica_groups=mesh['dp'=4,'expert'=32,'etp'=2] {'expert'}, dimensions={0} | all-to-all | bytes 12582912 | tf_op jit(solution)/shard_map/all_to_all | solution.py:62
  198.3 43.2 %all-gather.3.cloned.1.call-done = bf16[4,4096,768]{2,1,0:T(8,128)(2,1)} async-done(((bf16[4,1024,768]{2,1,0:T(8,128)(2,1)}), bf16[4,4096,768]{2,1,0:T(8,128)(2,1)}) %all-gather.3.cloned.1.call-update) | async-done | bytes 25165840 | tf_op jit(solution)/shard_map/all_gather | solution.py:26
  241.6 17.3 %fusion.2 = f32[2,384,768]{2,1,0:T(8,128)} fusion(bf16[4,4096,768]{2,1,0:T(8,128)(2,1)} %all-gather.3.cloned.1.call-done, bf16[2,384,4096]{2,0,1:T(2,128)(2,1)} %bitcast.50), kind=kOutput, calls=%fused_computation.2 | convolution fusion | flops 4831838208 | bytes 21233664 | tf_op jit(solution)/shard_map/erd,edf->erf/dot_general | solution.py:71
  258.9 16.0 %multiply_convert_fusion = bf16[2,384,768]{2,1,0:T(8,128)(2,1)} fusion(f32[2,384,768]{2,1,0:T(8,128)} %fusion.2, bf16[4,4096,768]{2,1,0:T(8,128)(2,1)} %all-gather.3.cloned.1.call-done, bf16[2,384,4096]{2,0,1:T(2,128)(2,1)S(1)} %bitcast.51), kind=kOutput, calls=%fused_computation.10 | convolution fusion | flops 4835377152 | bytes 22413312 | tf_op jit(solution)/shard_map/erd,edf->erf/dot_general | solution.py:72
  274.9 90.6 %all-gather.5.cloned.1.call-done = bf16[2,768,4096]{2,1,0:T(8,128)(2,1)} async-done(((bf16[2,768,1024]{2,1,0:T(8,128)(2,1)}), bf16[2,768,4096]{2,1,0:T(8,128)(2,1)}) %all-gather.5.cloned.1.call-update) | async-done | bytes 12582928 | tf_op jit(solution)/shard_map/all_gather | solution.py:77
  365.5 8.4 %convolution_convert_fusion = bf16[2,384,4096]{2,1,0:T(8,128)(2,1)S(1)} fusion(bf16[2,384,768]{2,1,0:T(8,128)(2,1)} %multiply_convert_fusion, bf16[2,768,4096]{2,1,0:T(8,128)(2,1)} %all-gather.5.cloned.1.call-done), kind=kOutput, calls=%fused_computation.4 | convolution fusion | flops 4834983936 | bytes 20054016 | tf_op jit(solution)/shard_map/erf,efd->erd/dot_general | solution.py:74
  373.9 1.1 copy.73
  375.0 10.0 %all_to_all.41 = bf16[2,2,384,2048]{3,2,1,0:T(8,128)(2,1)} all-to-all(bf16[2,2,384,2048]{3,2,1,0:T(8,128)(2,1)S(1)} %bitcast.47), channel_id=1, replica_groups=mesh['dp'=4,'expert'=32,'etp'=2] {'etp'}, dimensions={0} | all-to-all | bytes 12582912 | tf_op jit(solution)/shard_map/all_to_all | solution.py:37
  385.0 5.4 %reduce_sum.32 = bf16[2,384,2048]{2,1,0:T(8,128)(2,1)S(1)} reduce(bf16[2,2,384,2048]{3,2,1,0:T(8,128)(2,1)} %all_to_all.41, bf16[]{:T(256)} %constant.16.clone.1), dimensions={0}, to_apply=%region_5.6 | reduce | flops 1572864 | bytes 9437186 | tf_op jit(solution)/shard_map/reduce_sum | solution.py:38
  390.4 4.9 copy.59
  395.3 9.9 %all-to-all-start.3 = ((bf16[1,2,384,2048]{3,1,0,2:T(2,128)(2,1)}), bf16[1,2,384,2048]{3,1,0,2:T(2,128)(2,1)S(1)}, u32[]{:S(2)}, u32[]{:S(2)}) async-start(bf16[1,2,384,2048]{3,1,0,2:T(2,128)(2,1)} %copy.59), calls=%async_computation.3 | async-start | bytes 6291456 | tf_op jit(solution)/shard_map/all_to_all | solution.py:83
  406.0 74.4 %all-to-all-done.3 = bf16[1,2,384,2048]{3,1,0,2:T(2,128)(2,1)S(1)} async-done(((bf16[1,2,384,2048]{3,1,0,2:T(2,128)(2,1)}), bf16[1,2,384,2048]{3,1,0,2:T(2,128)(2,1)S(1)}, u32[]{:S(2)}, u32[]{:S(2)}) %all-to-all-start.3) | async-done | bytes 3145760 | tf_op jit(solution)/shard_map/all_to_all | solution.py:83
  480.3 3.5 copy.60
  483.9 4.7 reshape.42
  488.6 0.7 fusion.17
  489.2 1.4 fusion.6
  (28 shorter events, 2.4 us)
Async XLA Ops:
  6.5 235.0 %all-gather.3.cloned.1.call-start = ((), (), s32[]{:S(2)}) async-start(), calls=%async_computation.4 | async-start | bytes 31457280 | tf_op jit(solution)/shard_map/all_gather | solution.py:26
  12.6 1.0 copy-start.1
  12.6 5.3 %copy-start.2 = (s32[64,8]{0,1:T(8,128)S(1)}, s32[64,8]{0,1:T(8,128)}, u32[]{:S(2)}) copy-start(s32[64,8]{0,1:T(8,128)} %param.7) | copy-start | bytes 6148
  12.6 352.9 %all-gather.5.cloned.1.call-start = ((), (), s32[]{:S(2)}) async-start(), calls=%async_computation.5 | async-start | bytes 15728640 | tf_op jit(solution)/shard_map/all_gather | solution.py:77
  14.4 5.7 %all-to-all-start = ((bf16[2,64,2048]{2,1,0:T(8,128)(2,1)}), bf16[2,64,2048]{2,1,0:T(8,128)(2,1)S(1)}, u32[]{:S(2)}, u32[]{:S(2)}) async-start(bf16[2,64,2048]{2,1,0:T(8,128)(2,1)} %broadcast_in_dim.25), calls=%async_computation | async-start | bytes 1048576 | tf_op jit(solution)/shard_map/all_to_all | solution.py:9
  241.5 17.3 %copy-start = (bf16[32,2,12,4096]{3,1,2,0:T(2,128)(2,1)S(1)}, bf16[32,2,12,4096]{3,1,2,0:T(2,128)(2,1)}, u32[]{:S(2)}) copy-start(bf16[32,2,12,4096]{3,1,2,0:T(2,128)(2,1)} %all_to_all.40) | copy-start | bytes 18874372
  395.3 10.0 %copy-start.3 = (f32[64,8]{0,1:T(8,128)S(1)}, f32[64,8]{0,1:T(8,128)}, u32[]{:S(2)}) copy-start(f32[64,8]{0,1:T(8,128)} %param.8) | copy-start | bytes 6148
  395.3 85.0 %all-to-all-start.3 = ((bf16[1,2,384,2048]{3,1,0,2:T(2,128)(2,1)}), bf16[1,2,384,2048]{3,1,0,2:T(2,128)(2,1)S(1)}, u32[]{:S(2)}, u32[]{:S(2)}) async-start(bf16[1,2,384,2048]{3,1,0,2:T(2,128)(2,1)} %copy.59), calls=%async_computation.3 | async-start | bytes 6291456 | tf_op jit(solution)/shard_map/all_to_all | solution.py:83
Sparse Core Ops, SparseCore 0:
  12.7 228.8 all-gather.2
  243.4 122.0 all-gather.4
where the time goes:
time: 498 us; the launch traced here: 497 us
  waiting for transfers between devices  209 us (42%)
  blocking collectives  163 us (33%)
  matrix products  48.2 us (10%)
  local copies, waits for them, and re-layouts  36.3 us (7%)
  other arithmetic  13.9 us (3%)
  between operations  13.6 us (3%)
  starting transfers between devices  13.5 us (3%)
    all_to_all x1, blocking collectives, shards(): lax.all_to_all(packed.reshape(groups, held_count, capacity, gathered.shap...  153 us
    all_gather x1, waiting for transfers between devices, shards(): lax.all_gather(down_weight, 'dp', axis=2, tiled=True)  90.6 us
    all_to_all x1, waiting for transfers between devices, shards(): lax.all_to_all(expert_out[None], 'expert', split_axis=2, concat_axis=0, t...  74.4 us
    all_gather x1, waiting for transfers between devices, in_one_piece(): filled = lax.all_gather(both, axis, axis=dim, tiled=True)  43.2 us
    reshape x2, local copies, waits for them, and re-layouts, shards(): packed.reshape(groups, held_count, capacity, gathered.shape[1])  20.2 us
    dot_general x1, matrix products, shards(): jnp.einsum('erd,edf->erf', inputs, pieces[0], preferred_element_type=jnp....  17.3 us
    dot_general x1, matrix products, shards(): jnp.einsum('erd,edf->erf', inputs, pieces[1], preferred_element_type=jnp....  16 us
    all_to_all x1, blocking collectives, sum_at_owner(): lax.all_to_all(cut_along(shard, dim, count), axis, 0, 0, tiled=True)  9.99 us
  transfers between devices with their start and end apart: 4, of which 3 were waited for; matrix products, arithmetic and copies ran while one was open for 12% of the time, Pallas kernels for 0%

commit v1 on v0

--- a/solution.py
+++ b/solution.py
@@ -74,7 +74,9 @@
     partial_value = jnp.einsum(
         "erf,efd->erd",
         hidden,
-        lax.all_gather(down_weight, "dp", axis=2, tiled=True),
+        jnp.concatenate(
+            lax.all_to_all(jnp.stack([down_weight] * lax.axis_size("dp")), "dp", 0, 0), axis=2
+        ),
         preferred_element_type=jnp.float32,
     ).astype(jnp.bfloat16)
     partial_value = lax.optimization_barrier(partial_value)

time: 498 us -> 625 us (1.26)
  waiting for transfers between devices: 209 us -> 446 us
  blocking collectives: 163 us -> 15 us
  local copies, waits for them, and re-layouts: 36.3 us -> 53.6 us
  starting transfers between devices: 13.5 us -> 27.9 us
    all_to_all x1 -> x2, waiting for transfers between devices: 0.01 us -> 371 us  [the longest x1 244 us: shards(): lax.all_to_all(jnp.stack([down_weight] * lax.axis_size('dp')), 'dp', 0, 0)]
    all_to_all x1, blocking collectives: 153 us -> 5.03 us  [sent_to_all(): return lax.all_to_all(copies, axis, split_axis=0, concat_axis=0, tiled=True)]
    all_gather x1 -> x0, waiting for transfers between devices: 90.6 us -> none  [shards(): lax.all_gather(down_weight, 'dp', axis=2, tiled=True)]
    all_gather x1, waiting for transfers between devices: 43.2 us -> 0.01 us  [in_one_piece(): filled = lax.all_gather(both, axis, axis=dim, tiled=True)]
    all_to_all x1 -> x2, starting transfers between devices: 3.49 us -> 19.6 us  [the longest x1 9.84 us: shards(): lax.all_to_all(packed.reshape(groups, held_count, capacity, gathered.shap...]
    reshape x0 -> x1, local copies, waits for them, and re-layouts: none -> 10.7 us  [shards(): jnp.concatenate(lax.all_to_all(jnp.stack([down_weight] * lax.axis_size('d...]
    another operation x1 -> x2, local copies, waits for them, and re-layouts: 0.01 us -> 6.32 us  [the longest x1 6.32 us: shards(): jnp.stack([down_weight] * lax.axis_size('dp'))]
  transfers between devices with their start and end apart: 4 -> 4, of which waited for: 3 -> 3; matrix products, arithmetic and copies ran while one was open for 12% -> 7% of each run, Pallas kernels for 0% -> 0%
where the time goes in v1:
time: 625 us; the launch traced here: 622 us
  waiting for transfers between devices  446 us (71%)
  local copies, waits for them, and re-layouts  53.6 us (9%)
  matrix products  52.5 us (8%)
  starting transfers between devices  27.9 us (4%)
  blocking collectives  15 us (2%)
  other arithmetic  14 us (2%)
  between operations  13.5 us (2%)
    all_to_all x1, waiting for transfers between devices, shards(): lax.all_to_all(jnp.stack([down_weight] * lax.axis_size('dp')), 'dp', 0, 0)  244 us
    all_to_all x1, waiting for transfers between devices, shards(): lax.all_to_all(packed.reshape(groups, held_count, capacity, gathered.shap...  128 us
    all_to_all x1, waiting for transfers between devices, shards(): lax.all_to_all(expert_out[None], 'expert', split_axis=2, concat_axis=0, t...  74.2 us
    reshape x2, local copies, waits for them, and re-layouts, shards(): packed.reshape(groups, held_count, capacity, gathered.shape[1])  20.5 us
    dot_general x1, matrix products, shards(): jnp.einsum('erd,edf->erf', inputs, pieces[0], preferred_element_type=jnp....  19.2 us
    dot_general x1, matrix products, shards(): jnp.einsum('erd,edf->erf', inputs, pieces[1], preferred_element_type=jnp....  16.1 us
  transfers between devices with their start and end apart: 4, of which 3 were waited for; matrix products, arithmetic and copies ran while one was open for 7% of the time, Pallas kernels for 0%

profile of v1, /device:TPU:8, one launch (start us, length us, event | category | flops | bytes accessed | tf_op | source)
XLA Modules:
  0.0 622.1 jit_solution(11089278393356741661)
XLA Ops:
  6.5 6.1 pad_maximum_fusion
  13.6 5.0 all_to_all.45
  18.7 6.3 %stack.2 = bf16[4,2,768,1024]{3,2,1,0:T(8,128)(2,1)} broadcast(bf16[2,768,1024]{2,1,0:T(8,128)(2,1)S(1)} %copy-done), dimensions={1,2,3} | broadcast | bytes 15728640 | tf_op jit(solution)/shard_map/stack | solution.py:78
  25.0 9.8 %all-to-all-start.2 = ((bf16[4,2,768,1024]{3,2,1,0:T(8,128)(2,1)}), bf16[4,2,768,1024]{3,2,1,0:T(8,128)(2,1)}, u32[]{:S(2)}, u32[]{:S(2)}) async-start(bf16[4,2,768,1024]{3,2,1,0:T(8,128)(2,1)} %stack.2), calls=%async_computation.2 | async-start | bytes 25165824 | tf_op jit(solution)/shard_map/all_to_all | solution.py:78
  35.1 1.2 reduce-window.6
  37.5 4.6 convolution_convert_fusion.1
  42.2 9.9 %reshape.48 = bf16[32,2,12,4096]{3,2,1,0:T(8,128)(2,1)} reshape(bf16[768,4096]{1,0:T(8,128)(2,1)} %convolution_convert_fusion.1) | data formatting | bytes 12582912 | tf_op jit(solution)/shard_map/reshape | solution.py:63
  52.0 10.6 %copy.56 = bf16[32,2,12,4096]{3,1,2,0:T(2,128)(2,1)} copy(bf16[32,2,12,4096]{3,2,1,0:T(8,128)(2,1)} %reshape.48) | data formatting | bytes 12582912 | tf_op jit(solution)/shard_map/reshape | solution.py:63
  62.7 243.8 %all-to-all-done.2 = bf16[4,2,768,1024]{3,2,1,0:T(8,128)(2,1)} async-done(((bf16[4,2,768,1024]{3,2,1,0:T(8,128)(2,1)}), bf16[4,2,768,1024]{3,2,1,0:T(8,128)(2,1)}, u32[]{:S(2)}, u32[]{:S(2)}) %all-to-all-start.2) | async-done | bytes 12582944 | tf_op jit(solution)/shard_map/all_to_all | solution.py:78
  306.4 9.8 %all-to-all-start.1 = ((bf16[32,2,12,4096]{3,1,2,0:T(2,128)(2,1)}), bf16[32,2,12,4096]{3,1,2,0:T(2,128)(2,1)}, u32[]{:S(2)}, u32[]{:S(2)}) async-start(bf16[32,2,12,4096]{3,1,2,0:T(2,128)(2,1)} %copy.56), calls=%async_computation.1 | async-start | bytes 12582912 | tf_op jit(solution)/shard_map/all_to_all | solution.py:62
  316.3 10.7 %copy.68 = bf16[4,2,96,8,1024]{4,3,0,2,1:T(8,128)(2,1)} copy(bf16[4,2,96,8,1024]{4,3,2,1,0:T(8,128)(2,1)} %bitcast.19) | data formatting | bytes 25165824 | tf_op jit(solution)/shard_map/reshape | solution.py:77
  327.0 127.5 %all-to-all-done.1 = bf16[32,2,12,4096]{3,1,2,0:T(2,128)(2,1)} async-done(((bf16[32,2,12,4096]{3,1,2,0:T(2,128)(2,1)}), bf16[32,2,12,4096]{3,1,2,0:T(2,128)(2,1)}, u32[]{:S(2)}, u32[]{:S(2)}) %all-to-all-start.1) | async-done | bytes 6291488 | tf_op jit(solution)/shard_map/all_to_all | solution.py:62
  454.5 19.2 %fusion.2 = f32[2,384,768]{2,1,0:T(8,128)S(1)} fusion(bf16[4,4096,768]{2,1,0:T(8,128)(2,1)} %all-gather.2.cloned.1.call-done, bf16[2,384,4096]{2,0,1:T(2,128)(2,1)} %bitcast.4), kind=kOutput, calls=%fused_computation.2 | convolution fusion | flops 4831838208 | bytes 21233664 | tf_op jit(solution)/shard_map/erd,edf->erf/dot_general | solution.py:71
  473.7 16.1 %multiply_convert_fusion = bf16[2,384,768]{2,1,0:T(8,128)(2,1)S(1)} fusion(f32[2,384,768]{2,1,0:T(8,128)S(1)} %fusion.2, bf16[4,4096,768]{2,1,0:T(8,128)(2,1)} %all-gather.2.cloned.1.call-done, bf16[2,384,4096]{2,0,1:T(2,128)(2,1)} %bitcast.4), kind=kOutput, calls=%fused_computation.10 | convolution fusion | flops 4835377152 | bytes 22413312 | tf_op jit(solution)/shard_map/erd,edf->erf/dot_general | solution.py:72
  489.8 10.5 %convolution_convert_fusion = bf16[2,384,4096]{2,1,0:T(8,128)(2,1)S(1)} fusion(bf16[2,384,768]{2,1,0:T(8,128)(2,1)S(1)} %multiply_convert_fusion, bf16[2,768,4096]{2,1,0:T(8,128)(2,1)} %bitcast.50), kind=kOutput, calls=%fused_computation.4 | convolution fusion | flops 4834983936 | bytes 20054016 | tf_op jit(solution)/shard_map/erf,efd->erd/dot_general | solution.py:74
  500.3 1.1 copy.77
  501.4 10.0 %all_to_all.46 = bf16[2,2,384,2048]{3,2,1,0:T(8,128)(2,1)} all-to-all(bf16[2,2,384,2048]{3,2,1,0:T(8,128)(2,1)S(1)} %bitcast.51), channel_id=1, replica_groups=mesh['dp'=4,'expert'=32,'etp'=2] {'etp'}, dimensions={0} | all-to-all | bytes 12582912 | tf_op jit(solution)/shard_map/all_to_all | solution.py:37
  511.4 5.4 reduce_sum.32
  516.9 4.9 copy.62
  521.8 8.3 %all-to-all-start.4 = ((bf16[1,2,384,2048]{3,1,0,2:T(2,128)(2,1)}), bf16[1,2,384,2048]{3,1,0,2:T(2,128)(2,1)S(1)}, u32[]{:S(2)}, u32[]{:S(2)}) async-start(bf16[1,2,384,2048]{3,1,0,2:T(2,128)(2,1)} %copy.62), calls=%async_computation.4 | async-start | bytes 6291456 | tf_op jit(solution)/shard_map/all_to_all | solution.py:85
  530.7 74.2 %all-to-all-done.4 = bf16[1,2,384,2048]{3,1,0,2:T(2,128)(2,1)S(1)} async-done(((bf16[1,2,384,2048]{3,1,0,2:T(2,128)(2,1)}), bf16[1,2,384,2048]{3,1,0,2:T(2,128)(2,1)S(1)}, u32[]{:S(2)}, u32[]{:S(2)}) %all-to-all-start.4) | async-done | bytes 3145760 | tf_op jit(solution)/shard_map/all_to_all | solution.py:85
  604.9 3.5 copy.63
  608.5 4.7 reshape.52
  613.8 1.4 fusion.6
  (31 shorter events, 3.8 us)
Async XLA Ops:
  6.5 448.0 %all-gather.2.cloned.1.call-start = ((), (), s32[]{:S(2)}) async-start(), calls=%async_computation.5 | async-start | bytes 31457280 | tf_op jit(solution)/shard_map/all_gather | solution.py:26
  12.6 0.9 copy-start.2
  12.6 6.0 copy-start
  25.0 9.8 %copy-start.3 = (s32[64,8]{0,1:T(8,128)S(1)}, s32[64,8]{0,1:T(8,128)}, u32[]{:S(2)}) copy-start(s32[64,8]{0,1:T(8,128)} %param.7) | copy-start | bytes 6148
  25.0 11.9 %copy-start.1 = (bf16[2,64,2048]{2,1,0:T(8,128)(2,1)S(1)}, bf16[2,64,2048]{2,1,0:T(8,128)(2,1)}, u32[]{:S(2)}) copy-start(bf16[2,64,2048]{2,1,0:T(8,128)(2,1)} %all_to_all.45) | copy-start | bytes 1572868
  25.0 281.4 %all-to-all-start.2 = ((bf16[4,2,768,1024]{3,2,1,0:T(8,128)(2,1)}), bf16[4,2,768,1024]{3,2,1,0:T(8,128)(2,1)}, u32[]{:S(2)}, u32[]{:S(2)}) async-start(bf16[4,2,768,1024]{3,2,1,0:T(8,128)(2,1)} %stack.2), calls=%async_computation.2 | async-start | bytes 25165824 | tf_op jit(solution)/shard_map/all_to_all | solution.py:78
  306.4 148.1 %all-to-all-start.1 = ((bf16[32,2,12,4096]{3,1,2,0:T(2,128)(2,1)}), bf16[32,2,12,4096]{3,1,2,0:T(2,128)(2,1)}, u32[]{:S(2)}, u32[]{:S(2)}) async-start(bf16[32,2,12,4096]{3,1,2,0:T(2,128)(2,1)} %copy.56), calls=%async_computation.1 | async-start | bytes 12582912 | tf_op jit(solution)/shard_map/all_to_all | solution.py:62
  521.8 8.3 %copy-start.4 = (f32[64,8]{0,1:T(8,128)S(1)}, f32[64,8]{0,1:T(8,128)}, u32[]{:S(2)}) copy-start(f32[64,8]{0,1:T(8,128)} %param.8) | copy-start | bytes 6148
  521.8 83.2 %all-to-all-start.4 = ((bf16[1,2,384,2048]{3,1,0,2:T(2,128)(2,1)}), bf16[1,2,384,2048]{3,1,0,2:T(2,128)(2,1)S(1)}, u32[]{:S(2)}, u32[]{:S(2)}) async-start(bf16[1,2,384,2048]{3,1,0,2:T(2,128)(2,1)} %copy.62), calls=%async_computation.4 | async-start | bytes 6291456 | tf_op jit(solution)/shard_map/all_to_all | solution.py:85
Sparse Core Ops, SparseCore 0:
  12.8 361.8 all-gather.1
